TPU v7x, 32 devices: a whole 2x2x4 slice. The times are simulated.
32 devices in a mesh: band: 4 (over z), ga: 8 (over y, x, core).
Axes of the slice: x: 2, y: 2, z: 4, core: 2. Of those that a mesh axis runs over, the one named last changes fastest.
Arguments:
- waves: bfloat16 [2, 128, 8192], P(None, 'band', 'ga'), may hold values from -6 to 6
- occupations: float32 [128], P('band'), may hold values from 0.0015625 to 0.03125
- beta_table: float32 [72, 8192], P(None, 'ga'), may hold values from -0.046875 to 0.046875
- wave_miller: int32 [3, 8192], P(None, 'ga'), may hold values from 0 to 223
- atom_kinds: int32 [256], replicated, may hold values from 0 to 3
- atom_sites: int32 [3, 256], replicated, may hold values from 0 to 223
- aug_table: bfloat16 [684, 57344], P(None, ('band', 'ga')), may hold values from -0.00061035156 to 0.00061035156
- stick_columns: int32 [256], P(('band', 'ga')), may hold values from -1 to 14399, as said below
Outputs:
- density: float32 [2, 224, 240, 240], P(None, 'ga', 'band')
Inputs may be any that keep to these rules, and one draw needn't show every extreme that they name: `stick_columns`: entry t is a slot of the device at place t // 8 in band-major order, of band index t // 64. -1 marks an empty slot; otherwise the entry c names the column x = (t // 64) * 60 + c // 240, y = c mod 240. Live columns of one band index are distinct. On each device the live slots come first and at least one is live; in each band index some device has all 8 slots live.
All inputs are finite; a program needn't handle non-finite values.
Results may differ from a plain program's by a relative error of at most 0.0035.
Values sent between devices are 32-bit elements; how exact they have to be, the bound alone decides.
A program may use at most 64 MiB of HBM per device.

v0:
```python
import functools
import math

import jax
import jax.numpy as jnp
import numpy as np
from jax import lax
from jax.experimental import pallas as pl
from jax.experimental.pallas import tpu as pltpu
from jax.sharding import PartitionSpec as P

NX = 240
NY = 240
NZ = 224
NH = 18
HALF = NH // 2
SPECIES = 4

PERIOD = math.lcm(NX, NY, NZ)
STEP_X = PERIOD // NX
STEP_Y = PERIOD // NY
STEP_Z = PERIOD // NZ
ELL = np.array([0, 0] + [1] * 6 + [2] * 10)
PAIR_FIRST, PAIR_SECOND = np.triu_indices(NH)

highest = lax.Precision.HIGHEST
F32 = jnp.float32
BF16 = jnp.bfloat16


def fit_even(func, terms):
    nodes = 0.125 * (1.0 + np.cos(np.pi * (np.arange(64) + 0.5) / 64))
    scaled = np.polynomial.chebyshev.Chebyshev.fit(nodes, func(np.sqrt(nodes)), terms - 1, domain=[0, 0.25])
    return [float(c) for c in scaled.convert(kind=np.polynomial.Polynomial).coef]


COS_FIT = fit_even(lambda u: np.cos(2 * np.pi * u), 7)
SIN_FIT = fit_even(lambda u: np.sin(2 * np.pi * u) / u, 6)


def horner(coefs, w):
    total = jnp.full_like(w, coefs[-1])
    for c in coefs[-2::-1]:
        total = total * w + c
    return total


def turn_cos_sin(count, period):
    rest = count - jnp.round(count * (1.0 / period)) * period
    u = rest * (1.0 / period)
    w = u * u
    return horner(COS_FIT, w), u * horner(SIN_FIT, w)


MESH = pl.DeviceIdType.MESH


def greet(peers, axis_sets):
    barrier = pltpu.get_barrier_semaphore()
    for count, device_of in axis_sets:

        @pl.loop(1, count)
        def _(step):
            pl.semaphore_signal(barrier, inc=1, device_id=device_of(step), device_id_type=MESH)

    return lambda: pl.semaphore_wait(barrier, peers)


def up(value, unit):
    return -(-value // unit) * unit


def split(value):
    high = value.astype(BF16)
    return high, (value - high.astype(F32)).astype(BF16)


def mega_kernel(
    bands,
    groups,
    waves_ref,
    occ_ref,
    beta_ref,
    miller_ref,
    kinds_ref,
    site_ref,
    columns_ref,
    signs_ref,
    table_hbm,
    spread_hbm,
    out_ref,
    small_ref,
    site_t_ref,
    wave_ref,
    rows_ref,
    send_ref,
    recv_ref,
    phase_ref,
    total_ref,
    part_ref,
    band_ref,
    pair_ref,
    pack_ref,
    all_ref,
    weights_ref,
    table_ref,
    spread_ref,
    aug_ref,
    lines_ref,
    stick_ref,
    rs_send,
    rs_recv,
    band_send,
    band_recv,
    ga_send,
    ga_recv,
    dev_send,
    dev_recv,
    local_sem,
):
    band, me = lax.axis_index("band"), lax.axis_index("ga")
    devices = bands * groups
    place = band * groups + me
    atoms = site_ref.shape[1]
    own = atoms // groups
    width = miller_ref.shape[1]
    nb = waves_ref.shape[1]
    slots = columns_ref.shape[0]
    steps, _, block, cols = send_ref.shape
    ratio = block // own
    points = slots * NZ
    tile = phase_ref.shape[-1]
    planes = NZ // groups
    lanes = stick_ref.shape[-1]
    pairs = len(PAIR_FIRST)

    table_copy = pltpu.make_async_copy(table_hbm, table_ref, local_sem.at[0])
    spread_copy = pltpu.make_async_copy(spread_hbm, spread_ref, local_sem.at[1])
    table_copy.start()
    spread_copy.start()

    def peer(step):
        other = lax.rem(place + step, devices)
        return other // groups, lax.rem(other, groups)

    all_here = greet(devices - 1, [(devices, peer)])

    small_ref[...] = jnp.zeros_like(small_ref)
    small_ref[0:1, :] = site_ref[0:1, :].astype(F32) * STEP_X
    small_ref[1:2, :] = site_ref[1:2, :].astype(F32) * STEP_Y
    small_ref[2:3, :] = site_ref[2:3, :].astype(F32) * STEP_Z
    small_ref[3:4, :] = kinds_ref[...].astype(F32)
    small_ref[4:5, 0:nb] = occ_ref[...]
    small_ref[4:5, nb : 2 * nb] = occ_ref[...]
    site_t_ref[...] = jnp.swapaxes(small_ref[...], 0, 1)

    wave_ref[...] = jnp.zeros_like(wave_ref)
    re, im = waves_ref[0], waves_ref[1]
    for h in range(2):
        r, c = 2 * nb * h, 2 * width * h
        wave_ref[r : r + nb, c : c + width] = re
        wave_ref[r : r + nb, c + width : c + 2 * width] = im
        wave_ref[r + nb : r + 2 * nb, c : c + width] = im
        wave_ref[r + nb : r + 2 * nb, c + width : c + 2 * width] = -re

    def rs_copy(index, part, target, slot):
        return pltpu.make_async_remote_copy(
            src_ref=send_ref.at[index, :, pl.ds(pl.multiple_of(part * own, own), own), :],
            dst_ref=recv_ref.at[slot],
            send_sem=rs_send.at[target],
            recv_sem=rs_recv.at[slot],
            device_id=(band, target),
            device_id_type=MESH,
        )

    @pl.loop(0, steps)
    def _(step):
        index = lax.rem(me // ratio + 1 + step, steps)
        start = pl.multiple_of(index * block, block)
        site = site_t_ref[pl.ds(start, block), :]
        kinds = site[:, 3:4]
        miller = miller_ref[...].astype(F32)
        count = site[:, 0:1] * miller[0:1, :] + site[:, 1:2] * miller[1:2, :] + site[:, 2:3] * miller[2:3, :]
        cosine, sine = turn_cos_sin(count, PERIOD)
        masks = [kinds == float(s) for s in range(1, SPECIES)]
        for i in range(NH):
            radial = jnp.broadcast_to(beta_ref[i : i + 1, :], (block, width))
            for s in range(1, SPECIES):
                radial = jnp.where(masks[s - 1], beta_ref[s * NH + i : s * NH + i + 1, :], radial)
            if ELL[i] == 0:
                real, imag = radial * cosine, -(radial * sine)
            elif ELL[i] == 1:
                real, imag = -(radial * sine), -(radial * cosine)
            else:
                real, imag = -(radial * cosine), radial * sine
            row = (i % HALF) * block
            col = (i // HALF) * 2 * width
            rows_ref[row : row + block, col : col + width] = real.astype(BF16)
            rows_ref[row : row + block, col + width : col + 2 * width] = imag.astype(BF16)
        result = lax.dot_general(
            rows_ref[...], wave_ref[...], (((1,), (1,)), ((), ())), preferred_element_type=F32
        )
        send_ref[index] = result.reshape(HALF, block, cols)

        @pl.when(step == 0)
        def _():
            all_here()

        for part in range(ratio):
            target = index * ratio + part

            @pl.when(target != me)
            def _():
                rs_copy(index, part, target, me).start()

    @pl.loop(0, points // tile)
    def _(step):
        point = step * tile + lax.broadcasted_iota(jnp.int32, (1, tile), 1)
        x_row = jnp.zeros((1, tile), F32)
        y_row = jnp.zeros((1, tile), F32)
        z_row = point.astype(F32)
        for t in range(slots):
            column = columns_ref[t]
            x = band * (NX // bands) + lax.div(column, NY)
            y = lax.rem(column, NY)
            inside = point >= t * NZ
            x_row = jnp.where(inside, x.astype(F32), x_row)
            y_row = jnp.where(inside, y.astype(F32), y_row)
            z_row = jnp.where(inside, (point - t * NZ).astype(F32), z_row)
        count = site_t_ref[:, 0:1] * x_row + site_t_ref[:, 1:2] * y_row + site_t_ref[:, 2:3] * z_row
        cosine, sine = turn_cos_sin(count, PERIOD)
        phase_ref[step, 0] = cosine
        phase_ref[step, 1] = sine

    total = send_ref[me // ratio, :, pl.ds(pl.multiple_of(lax.rem(me, ratio) * own, own), own), :]
    for step in range(1, groups):
        source = lax.rem(me + step, groups)
        rs_copy(0, 0, source, source).wait_recv()
        total = total + recv_ref[source]

    total_ref[...] = jnp.zeros_like(total_ref)
    total_ref[0 : HALF * own, :] = total.reshape(HALF * own, cols)
    turned = jnp.swapaxes(total_ref[...], 0, 1)
    becp = jnp.concatenate([turned[0 : 2 * nb, : HALF * own], turned[2 * nb :, : HALF * own]], axis=1)
    scaled = becp * site_t_ref[0 : 2 * nb, 4:5]
    part_ref[...] = jnp.zeros_like(part_ref)
    for d in range(NH):
        size = (NH - d) * own
        product = scaled[:, :size] * becp[:, d * own :]
        part_ref[d : d + 1, 0:size] = jnp.sum(product, axis=0, keepdims=True)

    def band_copy(step, slot):
        return pltpu.make_async_remote_copy(
            src_ref=part_ref,
            dst_ref=band_ref.at[slot],
            send_sem=band_send.at[step],
            recv_sem=band_recv.at[slot],
            device_id=(lax.rem(band + step, bands), me),
            device_id_type=MESH,
        )

    for step in range(1, bands):
        band_copy(step, band).start()
    band_ref[band] = part_ref[...]
    for step in range(1, bands):
        band_copy(step, lax.rem(band + step, bands)).wait_recv()
    summed = band_ref[0]
    for source in range(1, bands):
        summed = summed + band_ref[source]

    pair_ref[...] = jnp.zeros_like(pair_ref)
    begin = 0
    for i in range(NH):
        pair_ref[begin : begin + NH - i, :] = summed[: NH - i, i * own : (i + 1) * own]
        begin += NH - i
    chunk = pack_ref.shape[0]
    chunks = pack_ref.shape[1] // own
    pack_ref[...] = jnp.concatenate(
        [pair_ref[q * chunk : (q + 1) * chunk, :] for q in range(chunks)], axis=1
    )

    def ga_copy(step, slot):
        return pltpu.make_async_remote_copy(
            src_ref=pack_ref,
            dst_ref=all_ref.at[slot],
            send_sem=ga_send.at[step],
            recv_sem=ga_recv.at[slot],
            device_id=(band, lax.rem(me + step, groups)),
            device_id_type=MESH,
        )

    for step in range(1, groups):
        ga_copy(step, me).start()
    all_ref[me] = pack_ref[...]
    for step in range(1, groups):
        ga_copy(step, lax.rem(me + step, groups)).wait_recv()
    becsum = jnp.concatenate(
        [
            jnp.concatenate([all_ref[g, :, q * own : (q + 1) * own] for g in range(groups)], axis=1)
            for q in range(chunks)
        ],
        axis=0,
    )[:pairs]
    even = becsum * signs_ref[:, 0:1]
    odd = becsum * signs_ref[:, 1:2]
    kind_row = small_ref[3:4, :]
    weights_ref[...] = jnp.zeros_like(weights_ref)
    for s in range(SPECIES):
        here = kind_row == float(s)
        weights_ref[s * pairs : (s + 1) * pairs, 0:atoms] = jnp.where(here, even, 0.0)
        weights_ref[s * pairs : (s + 1) * pairs, atoms : 2 * atoms] = jnp.where(here, odd, 0.0)
    weights = jnp.swapaxes(weights_ref[...], 0, 1).astype(BF16)[:, : SPECIES * pairs]

    table_copy.wait()
    for step in range(points // tile):
        coef = jnp.dot(
            weights, table_ref[:, step * tile : (step + 1) * tile], preferred_element_type=F32
        )
        real, imag = coef[:atoms], coef[atoms:]
        cosine, sine = phase_ref[step, 0], phase_ref[step, 1]
        aug_ref[0:1, step * tile : (step + 1) * tile] = jnp.sum(real * cosine + imag * sine, axis=0, keepdims=True)
        aug_ref[1:2, step * tile : (step + 1) * tile] = jnp.sum(imag * cosine - real * sine, axis=0, keepdims=True)

    lines_ref[...] = jnp.zeros_like(lines_ref)
    half = lines_ref.shape[1] // 2
    aug = aug_ref[...]
    for t in range(slots):
        lines_ref[t : t + 1, 0:NZ] = aug[0:1, t * NZ : (t + 1) * NZ]
        lines_ref[t : t + 1, half : half + NZ] = aug[1:2, t * NZ : (t + 1) * NZ]
    high, low = split(lines_ref[...])
    spread_copy.wait()
    lane = lax.broadcasted_iota(jnp.int32, (slots, lanes), 1)
    slot = lax.broadcasted_iota(jnp.int32, (slots, lanes), 0)
    marks = jnp.zeros((slots, lanes), F32)
    for t in range(slots):
        marks = jnp.where(slot == t, columns_ref[t].astype(F32), marks)
    both = jnp.concatenate([high, low], axis=0)
    packed = jnp.dot(both, spread_ref[0], preferred_element_type=F32)
    packed = packed[:slots] + packed[slots:] + jnp.dot(high, spread_ref[1], preferred_element_type=F32)
    for g in range(groups):
        stick_ref[g] = jnp.where(lane == 2 * planes, marks, packed[:, g * lanes : (g + 1) * lanes])

    def stick_copy(step, slot):
        target = peer(step)
        return pltpu.make_async_remote_copy(
            src_ref=stick_ref.at[target[1]],
            dst_ref=out_ref.at[slot],
            send_sem=dev_send.at[step],
            recv_sem=dev_recv.at[slot],
            device_id=target,
            device_id_type=MESH,
        )

    @pl.loop(1, devices)
    def _(step):
        stick_copy(step, place).start()

    out_ref[place] = stick_ref[me]

    @pl.loop(1, devices)
    def _(step):
        stick_copy(step, lax.rem(place + step, devices)).wait_recv()

    for step in range(1, groups):
        target = lax.rem(me + step, groups)
        rs_copy(0, 0, target, me).wait_send()
        ga_copy(step, me).wait_send()
    for step in range(1, bands):
        band_copy(step, band).wait_send()

    @pl.loop(1, devices)
    def _(step):
        stick_copy(step, place).wait_send()


def finish_kernel(bands, planes, received_ref, out_ref, table_ref, turned_ref, angle_ref, amp_ref):
    total, lanes = received_ref.shape
    batch = out_ref.shape[0]
    y_block = out_ref.shape[1]
    y_pad = angle_ref.shape[1]
    band = lax.axis_index("band")
    group = pl.program_id(0)

    @pl.when(group == 0)
    def _():
        received = received_ref[...]
        turned = jnp.swapaxes(received, 0, 1)
        turned_ref[...] = turned
        column_row = turned[2 * planes : 2 * planes + 1, :]
        live_row = column_row >= 0.0
        x_row = jnp.floor((column_row + 0.5) * (1.0 / NY))
        y_row = column_row - x_row * NY
        y_values = lax.broadcasted_iota(jnp.int32, (y_pad, total), 0) + band * y_block
        cos_y, sin_y = turn_cos_sin(y_values.astype(F32) * y_row, NY)
        angle_ref[0] = jnp.where(live_row, cos_y, 0.0)
        angle_ref[1] = jnp.where(live_row, sin_y, 0.0)
        column = received[:, 2 * planes : 2 * planes + 1]
        owner = lax.broadcasted_iota(jnp.int32, (total, 1), 0) // (total // bands)
        x = jnp.floor((column + 0.5) * (1.0 / NY)) + owner.astype(F32) * (NX // bands)
        x_values = lax.broadcasted_iota(jnp.int32, (total, 256), 1).astype(F32)
        cos_x, sin_x = turn_cos_sin(x * x_values, NX)
        for part, value in enumerate(split(cos_x)):
            table_ref[part, 0:total, 0:256] = value
            table_ref[part, total : 2 * total, 256:512] = value
        for part, value in enumerate(split(sin_x)):
            table_ref[part, 0:total, 256:512] = value
            table_ref[part, total : 2 * total, 0:256] = -value

    for k in range(batch):
        real = turned_ref[pl.ds(group * batch + k, 1), :]
        imag = turned_ref[pl.ds(planes + group * batch + k, 1), :]
        cosine, sine = angle_ref[0], angle_ref[1]
        row = k * y_pad
        amp_ref[row : row + y_pad, 0:total] = (real * cosine - imag * sine).astype(BF16)
        amp_ref[row : row + y_pad, total : 2 * total] = (real * sine + imag * cosine).astype(BF16)
    amp = amp_ref[...]
    for part in range(2):
        lane = slice(256 * part, 256 * part + 256)
        result = jnp.dot(amp, table_ref[0, :, lane], preferred_element_type=F32)
        result = result + jnp.dot(amp, table_ref[1, :, lane], preferred_element_type=F32)
        for k in range(batch):
            out_ref[k, :, part, :] = result[k * y_pad : k * y_pad + y_block, 0:NX]


def on_device(
    waves, occupations, beta_table, wave_miller, atom_kinds, atom_sites, aug_table, stick_columns
):
    bands = lax.axis_size("band")
    groups = lax.axis_size("ga")
    devices = bands * groups
    atoms = atom_sites.shape[1]
    slots = stick_columns.shape[0]
    nb = waves.shape[1]
    width = waves.shape[2]
    points = aug_table.shape[1]
    planes = NZ // groups
    pairs = len(PAIR_FIRST)
    own = atoms // groups
    block = own * max(1, 32 // own)
    steps = atoms // block
    cols = 4 * nb
    tile = math.gcd(points, 256)
    lanes = up(2 * planes + 1, 128)
    chunks = 128 // own
    chunk = up(-(-pairs // chunks), 8)

    odd = (ELL[PAIR_FIRST] + ELL[PAIR_SECOND]) % 2 == 1
    factors = np.where(PAIR_FIRST == PAIR_SECOND, 1.0, 2.0)
    signs = np.stack([np.where(odd, 0.0, factors), np.where(odd, -factors, 0.0)], axis=1).astype(np.float32)
    angle = (np.outer(np.arange(NZ), np.arange(NZ)) % NZ) * (2.0 * np.pi / NZ)
    cos_z = np.cos(angle).reshape(NZ, groups, planes)
    sin_z = np.sin(angle).reshape(NZ, groups, planes)
    half = up(NZ, 128)
    spread = np.zeros((2 * half, groups, lanes), np.float32)
    spread[:NZ, :, :planes] = cos_z
    spread[half : half + NZ, :, :planes] = -sin_z
    spread[:NZ, :, planes : 2 * planes] = sin_z
    spread[half : half + NZ, :, planes : 2 * planes] = cos_z
    spread = spread.reshape(2 * half, groups * lanes)
    spread_high = spread.astype(BF16)
    spread_low = (spread - spread_high.astype(np.float32)).astype(BF16)
    vmem = pl.BlockSpec(memory_space=pltpu.VMEM)
    hbm = pl.BlockSpec(memory_space=pl.ANY)
    dma = pltpu.SemaphoreType.DMA
    part_lanes = up(NH * own, 128)
    received = pl.pallas_call(
        functools.partial(mega_kernel, bands, groups),
        in_specs=[vmem] * 6 + [pl.BlockSpec(memory_space=pltpu.SMEM), vmem, hbm, hbm],
        out_specs=vmem,
        out_shape=jax.ShapeDtypeStruct((devices, slots, lanes), F32),
        scratch_shapes=[
            pltpu.VMEM((8, atoms), F32),
            pltpu.VMEM((atoms, 8), F32),
            pltpu.VMEM((cols, 4 * width), BF16),
            pltpu.VMEM((HALF * block, 4 * width), BF16),
            pltpu.VMEM((steps, HALF, block, cols), F32),
            pltpu.VMEM((groups, HALF, own, cols), F32),
            pltpu.VMEM((points // tile, 2, atoms, tile), F32),
            pltpu.VMEM((up(HALF * own, 128), cols), F32),
            pltpu.VMEM((up(NH, 8), part_lanes), F32),
            pltpu.VMEM((bands, up(NH, 8), part_lanes), F32),
            pltpu.VMEM((chunk * chunks, own), F32),
            pltpu.VMEM((chunk, chunks * own), F32),
            pltpu.VMEM((groups, chunk, chunks * own), F32),
            pltpu.VMEM((up(SPECIES * pairs, 128), 2 * atoms), F32),
            pltpu.VMEM(aug_table.shape, BF16),
            pltpu.VMEM((2,) + spread.shape, BF16),
            pltpu.VMEM((8, points), F32),
            pltpu.VMEM((slots, 2 * half), F32),
            pltpu.VMEM((groups, slots, lanes), F32),
            dma((groups,)),
            dma((groups,)),
            dma((bands,)),
            dma((bands,)),
            dma((groups,)),
            dma((groups,)),
            dma((devices,)),
            dma((devices,)),
            dma((2,)),
        ],
        compiler_params=pltpu.CompilerParams(collective_id=0, has_side_effects=True),
        name="slots",
    )(
        waves,
        occupations[None, :],
        beta_table,
        wave_miller,
        atom_kinds[None, :],
        atom_sites,
        stick_columns,
        jnp.asarray(signs),
        aug_table,
        jnp.asarray(np.stack([spread_high, spread_low])),
    )
    y_block = NY // bands
    total = devices * slots
    batch = math.gcd(planes, 7)
    y_pad = up(y_block, 16)
    result = pl.pallas_call(
        functools.partial(finish_kernel, bands, planes),
        grid=(planes // batch,),
        in_specs=[pl.BlockSpec((total, lanes), lambda g: (0, 0))],
        out_specs=pl.BlockSpec((batch, y_block, 2, NX), lambda g: (g, 0, 0, 0)),
        out_shape=jax.ShapeDtypeStruct((planes, y_block, 2, NX), F32),
        scratch_shapes=[
            pltpu.VMEM((2, 2 * total, 512), BF16),
            pltpu.VMEM((lanes, total), F32),
            pltpu.VMEM((2, y_pad, total), F32),
            pltpu.VMEM((batch * y_pad, 2 * total), BF16),
        ],
        name="finish",
    )(received.reshape(total, lanes))
    return result.transpose(2, 0, 1, 3)


def solution(mesh):
    in_specs = (
        P(None, "band", "ga"),
        P("band"),
        P(None, "ga"),
        P(None, "ga"),
        P(),
        P(),
        P(None, ("band", "ga")),
        P(("band", "ga")),
    )
    out_specs = P(None, "ga", "band", None)
    return jax.shard_map(
        on_device, mesh=mesh, in_specs=in_specs, out_specs=out_specs, check_vma=False
    )
```

profile of v0, /device:TPU:0, one launch (start us, length us, event | category | flops | bytes accessed | tf_op | source)
XLA Modules:
  0.0 48.1 jit_solution(8587447175069220448)
XLA Ops:
  0.0 42.4 %slots.1 = f32[32,8,128]{2,1,0:T(8,128)} custom-call(bf16[2,32,1024]{2,1,0:T(8,128)(2,1)} %waves_ref.1, f32[1,32]{1,0:T(1,128)} %bitcast.6, f32[72,1024]{1,0:T(8,128)} %beta_ref.1, s32[3,1024]{1,0:T(4,128)} %miller_ref.1, s32[1,256]{1,0:T(1,128)} %bitcast.5, s32[3,256]{1,0:T(4,128)} %site_ref.1, s32[8]{0:T(128)} %columns_ref.1, ...), custom_call_target="tpu_custom_call" | custom-call | tf_op jit(solution)/shard_map/slots/pallas_call | solution.py:466
  42.4 5.7 %finish.1 = f32[28,60,2,240]{3,2,1,0:T(2,128)} custom-call(f32[256,128]{1,0:T(8,128)} %bitcast.4), custom_call_target="tpu_custom_call" | custom-call | tf_op jit(solution)/shard_map/finish/pallas_call | solution.py:519
where the time goes:
time: 48.2 us; the launch traced here: 48.1 us
  Pallas kernels  48 us (100%)
    pallas_call x1, Pallas kernels, on_device(): pl.pallas_call(functools.partial(mega_kernel, bands, groups), in_specs=[v...  42.4 us
    pallas_call x1, Pallas kernels, on_device(): pl.pallas_call(functools.partial(finish_kernel, bands, planes), grid=(pla...  5.66 us

commit v1 on v0

v1 whole, which is shorter than its diff:
```python
import functools
import math

import jax
import jax.numpy as jnp
import numpy as np
from jax import lax
from jax.experimental import pallas as pl
from jax.experimental.pallas import tpu as pltpu
from jax.sharding import PartitionSpec as P

NX = 240
NY = 240
NZ = 224
NH = 18
HALF = NH // 2
SPECIES = 4

PERIOD = math.lcm(NX, NY, NZ)
STEP_X = PERIOD // NX
STEP_Y = PERIOD // NY
STEP_Z = PERIOD // NZ
ELL = np.array([0, 0] + [1] * 6 + [2] * 10)
PAIR_FIRST, PAIR_SECOND = np.triu_indices(NH)

highest = lax.Precision.HIGHEST
F32 = jnp.float32
BF16 = jnp.bfloat16


def fit_even(func, terms):
    nodes = 0.125 * (1.0 + np.cos(np.pi * (np.arange(64) + 0.5) / 64))
    scaled = np.polynomial.chebyshev.Chebyshev.fit(nodes, func(np.sqrt(nodes)), terms - 1, domain=[0, 0.25])
    return [float(c) for c in scaled.convert(kind=np.polynomial.Polynomial).coef]


COS_FIT = fit_even(lambda u: np.cos(2 * np.pi * u), 7)
SIN_FIT = fit_even(lambda u: np.sin(2 * np.pi * u) / u, 6)


def horner(coefs, w):
    total = jnp.full_like(w, coefs[-1])
    for c in coefs[-2::-1]:
        total = total * w + c
    return total


def turn_cos_sin(count, period):
    rest = count - jnp.round(count * (1.0 / period)) * period
    u = rest * (1.0 / period)
    w = u * u
    return horner(COS_FIT, w), u * horner(SIN_FIT, w)


MESH = pl.DeviceIdType.MESH


def greet(peers, axis_sets):
    barrier = pltpu.get_barrier_semaphore()
    for count, device_of in axis_sets:

        @pl.loop(1, count)
        def _(step):
            pl.semaphore_signal(barrier, inc=1, device_id=device_of(step), device_id_type=MESH)

    return lambda: pl.semaphore_wait(barrier, peers)


def up(value, unit):
    return -(-value // unit) * unit


def split(value):
    high = value.astype(BF16)
    return high, (value - high.astype(F32)).astype(BF16)


def mixed(value, other, count):
    if count & (count - 1):
        return lax.rem(value + other, count)
    total, bit = 0, 1
    while bit < count:
        total = total + lax.rem(value // bit + other // bit, 2) * bit
        bit *= 2
    return total


def mega_kernel(
    bands,
    groups,
    waves_hbm,
    occ_hbm,
    beta_hbm,
    miller_hbm,
    kinds_hbm,
    site_hbm,
    columns_hbm,
    signs_hbm,
    table_hbm,
    spread_hbm,
    out_ref,
    waves_ref,
    occ_ref,
    beta_ref,
    miller_ref,
    kinds_ref,
    site_ref,
    columns_ref,
    signs_ref,
    small_ref,
    site_t_ref,
    radial_ref,
    wave_ref,
    rows_ref,
    send_ref,
    mate_ref,
    recv_ref,
    phase_ref,
    total_ref,
    part_ref,
    band_ref,
    pair_ref,
    pack_ref,
    sum_ref,
    all_ref,
    weights_ref,
    table_ref,
    spread_ref,
    aug_ref,
    lines_ref,
    stick_ref,
    mate_send,
    mate_recv,
    rs_send,
    rs_recv,
    band_send,
    band_recv,
    ga_send,
    ga_recv,
    dev_send,
    dev_recv,
    local_sem,
):
    band, me = lax.axis_index("band"), lax.axis_index("ga")
    devices = bands * groups
    place = band * groups + me
    chips = groups // 2
    chip, core = me // 2, lax.rem(me, 2)
    atoms = site_ref.shape[1]
    own = atoms // groups
    width = miller_ref.shape[1]
    nb = waves_ref.shape[1]
    slots = columns_ref.shape[0]
    steps, _, block, cols = send_ref.shape
    ratio = block // own
    paired = ratio == 1
    rounds = steps // 2 if paired else steps
    units = max(1, ratio // 2)
    points = slots * NZ
    tile = phase_ref.shape[-1]
    planes = NZ // groups
    rows, lanes = stick_ref.shape[1:]
    span = lanes * rows // slots
    pairs = len(PAIR_FIRST)

    sources = (site_hbm, kinds_hbm, occ_hbm, waves_hbm, miller_hbm, beta_hbm, columns_hbm, signs_hbm, table_hbm, spread_hbm)
    targets = (site_ref, kinds_ref, occ_ref, waves_ref, miller_ref, beta_ref, columns_ref, signs_ref, table_ref, spread_ref)
    loads = [pltpu.make_async_copy(a, b, local_sem.at[n]) for n, (a, b) in enumerate(zip(sources, targets))]
    for load in loads:
        load.start()

    all_here = greet(
        groups - 1 + bands - 1,
        [
            (groups, lambda step: (band, lax.rem(me + step, groups))),
            (bands, lambda step: (lax.rem(band + step, bands), me)),
        ],
    )

    wave_ref[...] = jnp.zeros_like(wave_ref)
    small_ref[...] = jnp.zeros_like(small_ref)
    for load in loads[:3]:
        load.wait()
    small_ref[0:1, :] = site_ref[0:1, :].astype(F32) * STEP_X
    small_ref[1:2, :] = site_ref[1:2, :].astype(F32) * STEP_Y
    small_ref[2:3, :] = site_ref[2:3, :].astype(F32) * STEP_Z
    small_ref[3:4, :] = kinds_ref[...].astype(F32)
    small_ref[4:5, 0:nb] = occ_ref[...]
    small_ref[4:5, nb : 2 * nb] = occ_ref[...]
    site_t_ref[...] = jnp.swapaxes(small_ref[...], 0, 1)

    loads[3].wait()
    re, im = waves_ref[0], waves_ref[1]
    for h in range(2):
        r, c = 2 * nb * h, 2 * width * h
        wave_ref[r : r + nb, c : c + width] = re
        wave_ref[r : r + nb, c + width : c + 2 * width] = im
        wave_ref[r + nb : r + 2 * nb, c : c + width] = im
        wave_ref[r + nb : r + 2 * nb, c + width : c + 2 * width] = -re
    loads[4].wait()
    loads[5].wait()
    for i in range(NH):
        for s in range(SPECIES):
            row = (i // HALF) * SPECIES + s
            radial_ref[i % HALF, row : row + 1, :] = beta_ref[s * NH + i : s * NH + i + 1, :]

    def located(turn, unit, own_core):
        kind = core if own_core else 1 - core
        if paired:
            target = mixed(chip, rounds - 1 - turn, rounds) * 2 + kind
            return target, 0, target
        index = mixed(me // ratio, rounds - 1 - turn, rounds)
        part = 2 * unit + kind
        return index, pl.multiple_of(part * own, own), index * ratio + part

    def mate_copy(index, offset, slot):
        return pltpu.make_async_remote_copy(
            src_ref=send_ref.at[index, :, pl.ds(offset, own), :],
            dst_ref=mate_ref.at[slot],
            send_sem=mate_send.at[slot],
            recv_sem=mate_recv.at[slot],
            device_id=(band, chip * 2 + 1 - core),
            device_id_type=MESH,
        )

    def rs_copy(index, offset, target, slot):
        return pltpu.make_async_remote_copy(
            src_ref=send_ref.at[index, :, pl.ds(offset, own), :],
            dst_ref=recv_ref.at[slot],
            send_sem=rs_send.at[target],
            recv_sem=rs_recv.at[slot],
            device_id=(band, target * 2 + core),
            device_id_type=MESH,
        )

    def project(index):
        start = pl.multiple_of(index * block, block)
        site = site_t_ref[pl.ds(start, block), :]
        kinds = site[:, 3:4]
        miller = miller_ref[...].astype(F32)
        count = site[:, 0:1] * miller[0:1, :] + site[:, 1:2] * miller[1:2, :] + site[:, 2:3] * miller[2:3, :]
        cosine, sine = turn_cos_sin(count, PERIOD)
        minus = -sine
        kinds8 = [
            [jnp.broadcast_to(kinds[q : q + 8] + float(SPECIES * h), (8, width)).astype(jnp.int32) for q in range(0, block, 8)]
            for h in range(2)
        ]
        for i in range(NH):
            radial = jnp.concatenate(
                [
                    jnp.take_along_axis(
                        radial_ref[i % HALF],
                        kinds8[i // HALF][q],
                        axis=0,
                        mode="promise_in_bounds",
                    )
                    for q in range(block // 8)
                ],
                axis=0,
            )
            first, second = (sine, cosine) if ELL[i] == 1 else (cosine, minus)
            row = (i % HALF) * block
            col = (i // HALF) * 2 * width
            rows_ref[row : row + block, col : col + width] = (radial * first).astype(BF16)
            rows_ref[row : row + block, col + width : col + 2 * width] = (radial * second).astype(BF16)
        result = lax.dot_general(
            rows_ref[...], wave_ref[...], (((1,), (1,)), ((), ())), preferred_element_type=F32
        )
        send_ref[index] = result.reshape(HALF, block, cols)

    def forward(turn):
        for unit in range(units):
            index, offset, target = located(turn, unit, False)
            mate_copy(index, offset, target // 2).start()

    def settle(turn):
        for unit in range(units):
            index, offset, target = located(turn, unit, True)
            mate_copy(index, offset, target // 2).wait_recv()
            here = (index, slice(None), pl.ds(offset, own), slice(None))
            send_ref[here] = send_ref[here] + mate_ref[target // 2]

            @pl.when(target != me)
            def _():
                rs_copy(index, offset, target // 2, chip).start()

    @pl.loop(0, steps)
    def _(step):
        if paired:
            project(mixed(chip, rounds - 1 - step // 2, rounds) * 2 + lax.rem(core + 1 + step, 2))
        else:
            project(mixed(me // ratio, rounds - 1 - step, rounds))

        @pl.when(step == 0)
        def _():
            all_here()

        if paired:

            @pl.when(lax.rem(step, 2) == 0)
            def _():
                forward(step // 2)

            @pl.when((lax.rem(step, 2) == 0) & (step > 0))
            def _():
                settle(step // 2 - 1)

        else:
            forward(step)

            @pl.when(step > 0)
            def _():
                settle(step - 1)

    if not paired:
        settle(rounds - 1)

    loads[6].wait()

    @pl.loop(0, points // tile)
    def _(step):
        point = step * tile + lax.broadcasted_iota(jnp.int32, (1, tile), 1)
        x_row = jnp.zeros((1, tile), F32)
        y_row = jnp.zeros((1, tile), F32)
        z_row = point.astype(F32)
        for t in range(slots):
            column = columns_ref[t]
            x = band * (NX // bands) + lax.div(column, NY)
            y = lax.rem(column, NY)
            inside = point >= t * NZ
            x_row = jnp.where(inside, x.astype(F32), x_row)
            y_row = jnp.where(inside, y.astype(F32), y_row)
            z_row = jnp.where(inside, (point - t * NZ).astype(F32), z_row)
        count = site_t_ref[:, 0:1] * x_row + site_t_ref[:, 1:2] * y_row + site_t_ref[:, 2:3] * z_row
        cosine, sine = turn_cos_sin(count, PERIOD)
        phase_ref[step, 0] = cosine
        phase_ref[step, 1] = sine

    if paired:
        settle(rounds - 1)
    total = send_ref[me // ratio, :, pl.ds(pl.multiple_of(lax.rem(me, ratio) * own, own), own), :]
    for step in range(1, chips):
        source = lax.rem(chip + step, chips)
        rs_copy(0, 0, source, source).wait_recv()
        total = total + recv_ref[source]

    total_ref[...] = jnp.zeros_like(total_ref)
    total_ref[0 : HALF * own, :] = total.reshape(HALF * own, cols)
    turned = jnp.swapaxes(total_ref[...], 0, 1)
    becp = jnp.concatenate([turned[0 : 2 * nb, : HALF * own], turned[2 * nb :, : HALF * own]], axis=1)
    scaled = becp * site_t_ref[0 : 2 * nb, 4:5]
    for d in range(NH):
        size = (NH - d) * own
        product = scaled[:, :size] * becp[:, d * own :]
        part_ref[d : d + 1, 0:size] = jnp.sum(product, axis=0, keepdims=True)

    pair_ref[...] = jnp.zeros_like(pair_ref)
    begin = 0
    for i in range(NH):
        pair_ref[begin : begin + NH - i, :] = part_ref[: NH - i, i * own : (i + 1) * own]
        begin += NH - i
    chunk = pack_ref.shape[0]
    chunks = pack_ref.shape[1] // own
    pack_ref[...] = jnp.concatenate(
        [pair_ref[q * chunk : (q + 1) * chunk, :] for q in range(chunks)], axis=1
    )

    def band_copy(step, slot):
        return pltpu.make_async_remote_copy(
            src_ref=pack_ref,
            dst_ref=band_ref.at[slot],
            send_sem=band_send.at[step],
            recv_sem=band_recv.at[slot],
            device_id=(mixed(band, step, bands), me),
            device_id_type=MESH,
        )

    for step in range(bands - 1, 0, -1):
        band_copy(step, band).start()
    summed = pack_ref[...]
    for step in range(1, bands):
        source = lax.rem(band + step, bands)
        band_copy(step, source).wait_recv()
        summed = summed + band_ref[source]
    sum_ref[...] = summed

    def ga_copy(step, slot):
        return pltpu.make_async_remote_copy(
            src_ref=sum_ref,
            dst_ref=all_ref.at[slot],
            send_sem=ga_send.at[step],
            recv_sem=ga_recv.at[slot],
            device_id=(band, mixed(me, step, groups)),
            device_id_type=MESH,
        )

    for step in range(groups - 1, 0, -1):
        ga_copy(step, me).start()
    all_ref[me] = sum_ref[...]
    for step in range(1, groups):
        ga_copy(step, lax.rem(me + step, groups)).wait_recv()
    becsum = jnp.concatenate(
        [
            jnp.concatenate([all_ref[g, :, q * own : (q + 1) * own] for g in range(groups)], axis=1)
            for q in range(chunks)
        ],
        axis=0,
    )[:pairs]
    loads[7].wait()
    even = becsum * signs_ref[:, 0:1]
    odd = becsum * signs_ref[:, 1:2]
    kind_row = small_ref[3:4, :]
    weights_ref[...] = jnp.zeros_like(weights_ref)
    for s in range(SPECIES):
        here = kind_row == float(s)
        weights_ref[s * pairs : (s + 1) * pairs, 0:atoms] = jnp.where(here, even, 0.0)
        weights_ref[s * pairs : (s + 1) * pairs, atoms : 2 * atoms] = jnp.where(here, odd, 0.0)
    weights = jnp.swapaxes(weights_ref[...], 0, 1).astype(BF16)[:, : SPECIES * pairs]

    loads[8].wait()
    for step in range(points // tile):
        coef = jnp.dot(
            weights, table_ref[:, step * tile : (step + 1) * tile], preferred_element_type=F32
        )
        real, imag = coef[:atoms], coef[atoms:]
        cosine, sine = phase_ref[step, 0], phase_ref[step, 1]
        aug_ref[0:1, step * tile : (step + 1) * tile] = jnp.sum(real * cosine + imag * sine, axis=0, keepdims=True)
        aug_ref[1:2, step * tile : (step + 1) * tile] = jnp.sum(imag * cosine - real * sine, axis=0, keepdims=True)

    lines_ref[...] = jnp.zeros_like(lines_ref)
    half = lines_ref.shape[1] // 2
    aug = aug_ref[0:2, :]
    for t in range(slots):
        lines_ref[t : t + 1, 0:NZ] = aug[0:1, t * NZ : (t + 1) * NZ]
        lines_ref[t : t + 1, half : half + NZ] = aug[1:2, t * NZ : (t + 1) * NZ]
    high, low = split(lines_ref[...])
    loads[9].wait()
    lane = lax.broadcasted_iota(jnp.int32, (slots, groups * span), 1)
    slot = lax.broadcasted_iota(jnp.int32, (slots, groups * span), 0)
    marks = jnp.zeros((slots, groups * span), F32)
    for t in range(slots):
        marks = jnp.where(slot == t, columns_ref[t].astype(F32), marks)
    both = jnp.concatenate([high, low], axis=0)
    packed = jnp.dot(both, spread_ref[0], preferred_element_type=F32)
    packed = packed[:slots] + packed[slots:] + jnp.dot(high, spread_ref[1], preferred_element_type=F32)
    packed = jnp.where(lax.rem(lane, span) == 2 * planes, marks, packed)
    for g in range(groups):
        stick_ref[g] = jnp.concatenate(
            [packed[q * rows : (q + 1) * rows, g * span : (g + 1) * span] for q in range(slots // rows)], axis=1
        )

    def stick_copy(step, target, slot):
        return pltpu.make_async_remote_copy(
            src_ref=stick_ref.at[target[1]],
            dst_ref=out_ref.at[slot],
            send_sem=dev_send.at[step],
            recv_sem=dev_recv.at[slot],
            device_id=target,
            device_id_type=MESH,
        )

    @pl.loop(0, bands - 1)
    def _(turn):
        other = mixed(band, bands - 1 - turn, bands)
        for step in range(groups):
            stick_copy(turn * groups + step, (other, lax.rem(me + step, groups)), place).start()

    for step in range(1, groups):
        stick_copy((bands - 1) * groups + step, (band, lax.rem(me + step, groups)), place).start()

    out_ref[place] = stick_ref[me]

    @pl.loop(1, devices)
    def _(step):
        stick_copy(step, (band, me), lax.rem(place + step, devices)).wait_recv()

    for slot in range(chips):
        mate_copy(0, 0, slot).wait_send()
    for step in range(1, chips):
        rs_copy(0, 0, lax.rem(chip + step, chips), chip).wait_send()
    for step in range(1, groups):
        ga_copy(step, me).wait_send()
    for step in range(1, bands):
        band_copy(step, band).wait_send()

    @pl.loop(0, devices)
    def _(step):
        @pl.when(step != (bands - 1) * groups)
        def _():
            stick_copy(step, (band, me), place).wait_send()


def finish_kernel(bands, planes, span, received_ref, out_ref, table_ref, turned_ref, angle_ref, amp_ref):
    per_row = received_ref.shape[1] // span
    total = received_ref.shape[0] * per_row
    batch = out_ref.shape[0]
    y_block = out_ref.shape[1]
    y_pad = angle_ref.shape[1]
    band = lax.axis_index("band")
    group = pl.program_id(0)

    @pl.when(group == 0)
    def _():
        received = jnp.concatenate([received_ref[:, q * span : (q + 1) * span] for q in range(per_row)], axis=0)
        turned = jnp.swapaxes(received, 0, 1)
        turned_ref[...] = turned
        column_row = turned[2 * planes : 2 * planes + 1, :]
        live_row = column_row >= 0.0
        x_row = jnp.floor((column_row + 0.5) * (1.0 / NY))
        y_row = column_row - x_row * NY
        y_values = lax.broadcasted_iota(jnp.int32, (y_pad, total), 0) + band * y_block
        cos_y, sin_y = turn_cos_sin(y_values.astype(F32) * y_row, NY)
        angle_ref[0] = jnp.where(live_row, cos_y, 0.0)
        angle_ref[1] = jnp.where(live_row, sin_y, 0.0)
        column = received[:, 2 * planes : 2 * planes + 1]
        owner = lax.rem(lax.broadcasted_iota(jnp.int32, (total, 1), 0), total // per_row) // (total // per_row // bands)
        x = jnp.floor((column + 0.5) * (1.0 / NY)) + owner.astype(F32) * (NX // bands)
        x_values = lax.broadcasted_iota(jnp.int32, (total, 256), 1).astype(F32)
        cos_x, sin_x = turn_cos_sin(x * x_values, NX)
        for part, value in enumerate(split(cos_x)):
            table_ref[part, 0:total, 0:256] = value
            table_ref[part, total : 2 * total, 256:512] = value
        for part, value in enumerate(split(sin_x)):
            table_ref[part, 0:total, 256:512] = value
            table_ref[part, total : 2 * total, 0:256] = -value

    for k in range(batch):
        real = turned_ref[pl.ds(group * batch + k, 1), :]
        imag = turned_ref[pl.ds(planes + group * batch + k, 1), :]
        cosine, sine = angle_ref[0], angle_ref[1]
        row = k * y_pad
        amp_ref[row : row + y_pad, 0:total] = (real * cosine - imag * sine).astype(BF16)
        amp_ref[row : row + y_pad, total : 2 * total] = (real * sine + imag * cosine).astype(BF16)
    amp = amp_ref[...]
    for part in range(2):
        lane = slice(256 * part, 256 * part + 256)
        result = jnp.dot(amp, table_ref[0, :, lane], preferred_element_type=F32)
        result = result + jnp.dot(amp, table_ref[1, :, lane], preferred_element_type=F32)
        for k in range(batch):
            out_ref[k, :, part, :] = result[k * y_pad : k * y_pad + y_block, 0:NX]


def on_device(
    waves, occupations, beta_table, wave_miller, atom_kinds, atom_sites, aug_table, stick_columns
):
    bands = lax.axis_size("band")
    groups = lax.axis_size("ga")
    devices = bands * groups
    atoms = atom_sites.shape[1]
    slots = stick_columns.shape[0]
    nb = waves.shape[1]
    width = waves.shape[2]
    points = aug_table.shape[1]
    planes = NZ // groups
    pairs = len(PAIR_FIRST)
    own = atoms // groups
    block = own * max(1, 32 // own)
    steps = atoms // block
    cols = 4 * nb
    tile = math.gcd(points, 256)
    lanes = 128
    span = next(n for n in (16, 32, 64, 128) if n >= 2 * planes + 1 and n * slots >= lanes)
    stick_rows = slots * span // lanes
    chunks = 128 // own
    chunk = up(-(-pairs // chunks), 8)

    odd = (ELL[PAIR_FIRST] + ELL[PAIR_SECOND]) % 2 == 1
    factors = np.where(PAIR_FIRST == PAIR_SECOND, 1.0, 2.0)
    factors = np.where((ELL[PAIR_FIRST] == 0) != (ELL[PAIR_SECOND] == 0), -factors, factors)
    signs = np.stack([np.where(odd, 0.0, factors), np.where(odd, -factors, 0.0)], axis=1).astype(np.float32)
    angle = (np.outer(np.arange(NZ), np.arange(NZ)) % NZ) * (2.0 * np.pi / NZ)
    cos_z = np.cos(angle).reshape(NZ, groups, planes)
    sin_z = np.sin(angle).reshape(NZ, groups, planes)
    half = up(NZ, 128)
    spread = np.zeros((2 * half, groups, span), np.float32)
    spread[:NZ, :, :planes] = cos_z
    spread[half : half + NZ, :, :planes] = -sin_z
    spread[:NZ, :, planes : 2 * planes] = sin_z
    spread[half : half + NZ, :, planes : 2 * planes] = cos_z
    spread = spread.reshape(2 * half, groups * span)
    spread_high = spread.astype(BF16)
    spread_low = (spread - spread_high.astype(np.float32)).astype(BF16)
    vmem = pl.BlockSpec(memory_space=pltpu.VMEM)
    hbm = pl.BlockSpec(memory_space=pl.ANY)
    dma = pltpu.SemaphoreType.DMA
    part_lanes = up(NH * own, 128)
    inputs = (
        waves,
        occupations[None, :],
        beta_table,
        wave_miller,
        atom_kinds[None, :],
        atom_sites,
        stick_columns,
        jnp.asarray(signs),
        aug_table,
        jnp.asarray(np.stack([spread_high, spread_low])),
    )
    chips = groups // 2
    received = pl.pallas_call(
        functools.partial(mega_kernel, bands, groups),
        in_specs=[hbm] * len(inputs),
        out_specs=vmem,
        out_shape=jax.ShapeDtypeStruct((devices, stick_rows, lanes), F32),
        scratch_shapes=[
            pltpu.VMEM(waves.shape, BF16),
            pltpu.VMEM((1, nb), F32),
            pltpu.VMEM(beta_table.shape, F32),
            pltpu.VMEM(wave_miller.shape, jnp.int32),
            pltpu.VMEM((1, atoms), jnp.int32),
            pltpu.VMEM(atom_sites.shape, jnp.int32),
            pltpu.SMEM((slots,), jnp.int32),
            pltpu.VMEM(signs.shape, F32),
            pltpu.VMEM((8, atoms), F32),
            pltpu.VMEM((atoms, 8), F32),
            pltpu.VMEM((HALF, 2 * SPECIES, width), F32),
            pltpu.VMEM((cols, 4 * width), BF16),
            pltpu.VMEM((HALF * block, 4 * width), BF16),
            pltpu.VMEM((steps, HALF, block, cols), F32),
            pltpu.VMEM((chips, HALF, own, cols), F32),
            pltpu.VMEM((chips, HALF, own, cols), F32),
            pltpu.VMEM((points // tile, 2, atoms, tile), F32),
            pltpu.VMEM((up(HALF * own, 128), cols), F32),
            pltpu.VMEM((up(NH, 8), part_lanes), F32),
            pltpu.VMEM((bands, chunk, chunks * own), F32),
            pltpu.VMEM((chunk * chunks, own), F32),
            pltpu.VMEM((chunk, chunks * own), F32),
            pltpu.VMEM((chunk, chunks * own), F32),
            pltpu.VMEM((groups, chunk, chunks * own), F32),
            pltpu.VMEM((up(SPECIES * pairs, 128), 2 * atoms), F32),
            pltpu.VMEM(aug_table.shape, BF16),
            pltpu.VMEM((2,) + spread.shape, BF16),
            pltpu.VMEM((8, points), F32),
            pltpu.VMEM((slots, 2 * half), F32),
            pltpu.VMEM((groups, stick_rows, lanes), F32),
            dma((chips,)),
            dma((chips,)),
            dma((chips,)),
            dma((chips,)),
            dma((bands,)),
            dma((bands,)),
            dma((groups,)),
            dma((groups,)),
            dma((devices,)),
            dma((devices,)),
            dma((len(inputs),)),
        ],
        compiler_params=pltpu.CompilerParams(collective_id=0, has_side_effects=True),
        name="slots",
    )(*inputs)
    y_block = NY // bands
    total = devices * slots
    batch = math.gcd(planes, 7)
    y_pad = up(y_block, 16)
    result = pl.pallas_call(
        functools.partial(finish_kernel, bands, planes, span),
        grid=(planes // batch,),
        in_specs=[pl.BlockSpec((devices * stick_rows, lanes), lambda g: (0, 0))],
        out_specs=pl.BlockSpec((batch, y_block, 2, NX), lambda g: (g, 0, 0, 0)),
        out_shape=jax.ShapeDtypeStruct((planes, y_block, 2, NX), F32),
        scratch_shapes=[
            pltpu.VMEM((2, 2 * total, 512), BF16),
            pltpu.VMEM((span, total), F32),
            pltpu.VMEM((2, y_pad, total), F32),
            pltpu.VMEM((batch * y_pad, 2 * total), BF16),
        ],
        name="finish",
    )(received.reshape(devices * stick_rows, lanes))
    return result.transpose(2, 0, 1, 3)


def solution(mesh):
    in_specs = (
        P(None, "band", "ga"),
        P("band"),
        P(None, "ga"),
        P(None, "ga"),
        P(),
        P(),
        P(None, ("band", "ga")),
        P(("band", "ga")),
    )
    out_specs = P(None, "ga", "band", None)
    return jax.shard_map(
        on_device, mesh=mesh, in_specs=in_specs, out_specs=out_specs, check_vma=False
    )
```

time: 48.2 us -> 40 us (0.83)
  Pallas kernels: 48 us -> 39.8 us
    pallas_call x2, Pallas kernels: 48 us -> 39.8 us  [the longest x1 34.2 us: on_device(): pl.pallas_call(functools.partial(mega_kernel, bands, groups), in_specs=[h...]
where the time goes in v1:
time: 40 us; the launch traced here: 39.8 us
  Pallas kernels  39.8 us (99%)
    pallas_call x1, Pallas kernels, on_device(): pl.pallas_call(functools.partial(mega_kernel, bands, groups), in_specs=[h...  34.2 us
    pallas_call x1, Pallas kernels, on_device(): pl.pallas_call(functools.partial(finish_kernel, bands, planes, span), gri...  5.61 us

profile of v1, /device:TPU:0, one launch (start us, length us, event | category | flops | bytes accessed | tf_op | source)
XLA Modules:
  0.0 39.8 jit_solution(8027528199102667710)
XLA Ops:
  0.0 34.2 %slots.1 = f32[32,4,128]{2,1,0:T(4,128)} custom-call(bf16[2,32,1024]{2,1,0:T(8,128)(2,1)} %waves_hbm.1, f32[1,32]{1,0:T(1,128)} %bitcast.6, f32[72,1024]{1,0:T(8,128)} %beta_hbm.1, s32[3,1024]{1,0:T(4,128)} %miller_hbm.1, s32[1,256]{1,0:T(1,128)} %bitcast.5, s32[3,256]{1,0:T(4,128)} %site_hbm.1, s32[8]{0:T(128)} %columns_hbm.1, ...), custom_call_target="tpu_custom_call" | custom-call | tf_op jit(solution)/shard_map/slots/pallas_call | solution.py:600
  34.2 5.6 %finish.1 = f32[28,60,2,240]{3,2,1,0:T(2,128)} custom-call(f32[128,128]{1,0:T(8,128)} %bitcast.4), custom_call_target="tpu_custom_call" | custom-call | tf_op jit(solution)/shard_map/finish/pallas_call | solution.py:655

commit v2 on v1

--- a/solution.py
+++ b/solution.py
@@ -111,6 +111,9 @@
     site_t_ref,
     radial_ref,
     wave_ref,
+    wide_ref,
+    kind_ref,
+    turn_ref,
     rows_ref,
     send_ref,
     mate_ref,
@@ -129,16 +132,9 @@
     aug_ref,
     lines_ref,
     stick_ref,
-    mate_send,
     mate_recv,
-    rs_send,
-    rs_recv,
-    band_send,
-    band_recv,
-    ga_send,
-    ga_recv,
-    dev_send,
-    dev_recv,
+    sent,
+    came,
     local_sem,
 ):
     band, me = lax.axis_index("band"), lax.axis_index("ga")
@@ -188,6 +184,10 @@
     small_ref[4:5, 0:nb] = occ_ref[...]
     small_ref[4:5, nb : 2 * nb] = occ_ref[...]
     site_t_ref[...] = jnp.swapaxes(small_ref[...], 0, 1)
+    for n in range(3):
+        wide_ref[n] = jnp.broadcast_to(site_t_ref[:, n : n + 1], (atoms, 128))
+    kinds = jnp.broadcast_to(site_t_ref[:, 3:4], (atoms, 128)).astype(jnp.int32)
+    kind_ref[0], kind_ref[1] = kinds, kinds + SPECIES
 
     loads[3].wait()
     re, im = waves_ref[0], waves_ref[1]
@@ -213,59 +213,72 @@
         part = 2 * unit + kind
         return index, pl.multiple_of(part * own, own), index * ratio + part
 
+    def all_of(kind, ref, count):
+        return pltpu.make_async_remote_copy(
+            src_ref=ref.at[pl.ds(0, count)],
+            dst_ref=ref.at[pl.ds(0, count)],
+            send_sem=sent.at[kind],
+            recv_sem=came.at[kind],
+            device_id=(band, me),
+            device_id_type=MESH,
+        )
+
     def mate_copy(index, offset, slot):
         return pltpu.make_async_remote_copy(
             src_ref=send_ref.at[index, :, pl.ds(offset, own), :],
             dst_ref=mate_ref.at[slot],
-            send_sem=mate_send.at[slot],
+            send_sem=sent.at[0],
             recv_sem=mate_recv.at[slot],
             device_id=(band, chip * 2 + 1 - core),
             device_id_type=MESH,
         )
 
-    def rs_copy(index, offset, target, slot):
+    def rs_copy(index, offset, target):
         return pltpu.make_async_remote_copy(
             src_ref=send_ref.at[index, :, pl.ds(offset, own), :],
-            dst_ref=recv_ref.at[slot],
-            send_sem=rs_send.at[target],
-            recv_sem=rs_recv.at[slot],
+            dst_ref=recv_ref.at[chip],
+            send_sem=sent.at[1],
+            recv_sem=came.at[1],
             device_id=(band, target * 2 + core),
             device_id_type=MESH,
         )
 
-    def project(index):
+    def block_at(step):
+        if paired:
+            return mixed(chip, rounds - 1 - step // 2, rounds) * 2 + lax.rem(core + 1 + step, 2)
+        return mixed(me // ratio, rounds - 1 - step, rounds)
+
+    def turns(index):
+        sites = [wide_ref[n, pl.ds(pl.multiple_of(index * block, block), block), :] for n in range(3)]
+        sites = [jnp.concatenate([site] * (width // 128), axis=1) for site in sites]
+        miller = miller_ref[...].astype(F32)
+        count = sites[0] * miller[0:1, :] + sites[1] * miller[1:2, :] + sites[2] * miller[2:3, :]
+        cosine, sine = turn_cos_sin(count, PERIOD)
+        turn_ref[0], turn_ref[1], turn_ref[2] = cosine, -sine, sine
+
+    def project(index, after):
         start = pl.multiple_of(index * block, block)
-        site = site_t_ref[pl.ds(start, block), :]
-        kinds = site[:, 3:4]
-        miller = miller_ref[...].astype(F32)
-        count = site[:, 0:1] * miller[0:1, :] + site[:, 1:2] * miller[1:2, :] + site[:, 2:3] * miller[2:3, :]
-        cosine, sine = turn_cos_sin(count, PERIOD)
-        minus = -sine
-        kinds8 = [
-            [jnp.broadcast_to(kinds[q : q + 8] + float(SPECIES * h), (8, width)).astype(jnp.int32) for q in range(0, block, 8)]
-            for h in range(2)
+        kinds = [
+            [kind_ref[h, pl.ds(start + q, 8), :] for q in range(0, block, 8)] for h in range(2)
         ]
+        kinds = [[jnp.concatenate([kind] * (width // 128), axis=1) for kind in half] for half in kinds]
         for i in range(NH):
             radial = jnp.concatenate(
                 [
-                    jnp.take_along_axis(
-                        radial_ref[i % HALF],
-                        kinds8[i // HALF][q],
-                        axis=0,
-                        mode="promise_in_bounds",
-                    )
-                    for q in range(block // 8)
+                    jnp.take_along_axis(radial_ref[i % HALF], kind, axis=0, mode="promise_in_bounds")
+                    for kind in kinds[i // HALF]
                 ],
                 axis=0,
             )
-            first, second = (sine, cosine) if ELL[i] == 1 else (cosine, minus)
+            first, second = (2, 0) if ELL[i] == 1 else (0, 1)
             row = (i % HALF) * block
             col = (i // HALF) * 2 * width
-            rows_ref[row : row + block, col : col + width] = (radial * first).astype(BF16)
-            rows_ref[row : row + block, col + width : col + 2 * width] = (radial * second).astype(BF16)
+            rows_ref[row : row + block, col : col + width] = (radial * turn_ref[first]).astype(BF16)
+            rows_ref[row : row + block, col + width : col + 2 * width] = (radial * turn_ref[second]).astype(BF16)
         result = lax.dot_general(
             rows_ref[...], wave_ref[...], (((1,), (1,)), ((), ())), preferred_element_type=F32
         )
+        turns(after)
         send_ref[index] = result.reshape(HALF, block, cols)
 
     def forward(turn):
@@ -282,14 +295,13 @@
 
             @pl.when(target != me)
             def _():
-                rs_copy(index, offset, target // 2, chip).start()
+                rs_copy(index, offset, target // 2).start()
+
+    turns(block_at(0))
 
     @pl.loop(0, steps)
     def _(step):
-        if paired:
-            project(mixed(chip, rounds - 1 - step // 2, rounds) * 2 + lax.rem(core + 1 + step, 2))
-        else:
-            project(mixed(me // ratio, rounds - 1 - step, rounds))
+        project(block_at(step), block_at(lax.rem(step + 1, steps)))
 
         @pl.when(step == 0)
         def _():
@@ -301,9 +313,9 @@
             def _():
                 forward(step // 2)
 
-            @pl.when((lax.rem(step, 2) == 0) & (step > 0))
+            @pl.when((lax.rem(step, 2) == 1) & (step < steps - 1))
             def _():
-                settle(step // 2 - 1)
+                settle(step // 2)
 
         else:
             forward(step)
@@ -339,10 +351,9 @@
     if paired:
         settle(rounds - 1)
     total = send_ref[me // ratio, :, pl.ds(pl.multiple_of(lax.rem(me, ratio) * own, own), own), :]
+    all_of(1, recv_ref, chips - 1).wait_recv()
     for step in range(1, chips):
-        source = lax.rem(chip + step, chips)
-        rs_copy(0, 0, source, source).wait_recv()
-        total = total + recv_ref[source]
+        total = total + recv_ref[lax.rem(chip + step, chips)]
 
     total_ref[...] = jnp.zeros_like(total_ref)
     total_ref[0 : HALF * own, :] = total.reshape(HALF * own, cols)
@@ -365,40 +376,38 @@
         [pair_ref[q * chunk : (q + 1) * chunk, :] for q in range(chunks)], axis=1
     )
 
-    def band_copy(step, slot):
+    def band_copy(step):
         return pltpu.make_async_remote_copy(
             src_ref=pack_ref,
-            dst_ref=band_ref.at[slot],
-            send_sem=band_send.at[step],
-            recv_sem=band_recv.at[slot],
+            dst_ref=band_ref.at[band],
+            send_sem=sent.at[2],
+            recv_sem=came.at[2],
             device_id=(mixed(band, step, bands), me),
             device_id_type=MESH,
         )
 
     for step in range(bands - 1, 0, -1):
-        band_copy(step, band).start()
+        band_copy(step).start()
     summed = pack_ref[...]
+    all_of(2, band_ref, bands - 1).wait_recv()
     for step in range(1, bands):
-        source = lax.rem(band + step, bands)
-        band_copy(step, source).wait_recv()
-        summed = summed + band_ref[source]
+        summed = summed + band_ref[lax.rem(band + step, bands)]
     sum_ref[...] = summed
 
-    def ga_copy(step, slot):
+    def ga_copy(step):
         return pltpu.make_async_remote_copy(
             src_ref=sum_ref,
-            dst_ref=all_ref.at[slot],
-            send_sem=ga_send.at[step],
-            recv_sem=ga_recv.at[slot],
+            dst_ref=all_ref.at[me],
+            send_sem=sent.at[3],
+            recv_sem=came.at[3],
             device_id=(band, mixed(me, step, groups)),
             device_id_type=MESH,
         )
 
     for step in range(groups - 1, 0, -1):
-        ga_copy(step, me).start()
+        ga_copy(step).start()
     all_ref[me] = sum_ref[...]
-    for step in range(1, groups):
-        ga_copy(step, lax.rem(me + step, groups)).wait_recv()
+    all_of(3, all_ref, groups - 1).wait_recv()
     becsum = jnp.concatenate(
         [
             jnp.concatenate([all_ref[g, :, q * own : (q + 1) * own] for g in range(groups)], axis=1)
@@ -449,12 +458,12 @@
             [packed[q * rows : (q + 1) * rows, g * span : (g + 1) * span] for q in range(slots // rows)], axis=1
         )
 
-    def stick_copy(step, target, slot):
+    def stick_copy(target):
         return pltpu.make_async_remote_copy(
             src_ref=stick_ref.at[target[1]],
-            dst_ref=out_ref.at[slot],
-            send_sem=dev_send.at[step],
-            recv_sem=dev_recv.at[slot],
+            dst_ref=out_ref.at[place],
+            send_sem=sent.at[4],
+            recv_sem=came.at[4],
             device_id=target,
             device_id_type=MESH,
         )
@@ -463,36 +472,26 @@
     def _(turn):
         other = mixed(band, bands - 1 - turn, bands)
         for step in range(groups):
-            stick_copy(turn * groups + step, (other, lax.rem(me + step, groups)), place).start()
+            stick_copy((other, lax.rem(me + step, groups))).start()
 
     for step in range(1, groups):
-        stick_copy((bands - 1) * groups + step, (band, lax.rem(me + step, groups)), place).start()
+        stick_copy((band, lax.rem(me + step, groups))).start()
 
     out_ref[place] = stick_ref[me]
 
-    @pl.loop(1, devices)
-    def _(step):
-        stick_copy(step, (band, me), lax.rem(place + step, devices)).wait_recv()
-
-    for slot in range(chips):
-        mate_copy(0, 0, slot).wait_send()
-    for step in range(1, chips):
-        rs_copy(0, 0, lax.rem(chip + step, chips), chip).wait_send()
-    for step in range(1, groups):
-        ga_copy(step, me).wait_send()
-    for step in range(1, bands):
-        band_copy(step, band).wait_send()
-
-    @pl.loop(0, devices)
-    def _(step):
-        @pl.when(step != (bands - 1) * groups)
-        def _():
-            stick_copy(step, (band, me), place).wait_send()
+    all_of(4, out_ref, devices - 1).wait_recv()
+
+    all_of(0, mate_ref, chips).wait_send()
+    all_of(1, recv_ref, chips - 1).wait_send()
+    all_of(2, band_ref, bands - 1).wait_send()
+    all_of(3, all_ref, groups - 1).wait_send()
+    all_of(4, out_ref, devices - 1).wait_send()
 
 
 def finish_kernel(bands, planes, span, received_ref, out_ref, table_ref, turned_ref, angle_ref, amp_ref):
-    per_row = received_ref.shape[1] // span
-    total = received_ref.shape[0] * per_row
+    senders, stick_rows, lanes = received_ref.shape
+    per_row = lanes // span
+    total = senders * stick_rows * per_row
     batch = out_ref.shape[0]
     y_block = out_ref.shape[1]
     y_pad = angle_ref.shape[1]
@@ -501,7 +500,8 @@
 
     @pl.when(group == 0)
     def _():
-        received = jnp.concatenate([received_ref[:, q * span : (q + 1) * span] for q in range(per_row)], axis=0)
+        received = received_ref[...].reshape(senders * stick_rows, lanes)
+        received = jnp.concatenate([received[:, q * span : (q + 1) * span] for q in range(per_row)], axis=0)
         turned = jnp.swapaxes(received, 0, 1)
         turned_ref[...] = turned
         column_row = turned[2 * planes : 2 * planes + 1, :]
@@ -517,12 +517,11 @@
         x = jnp.floor((column + 0.5) * (1.0 / NY)) + owner.astype(F32) * (NX // bands)
         x_values = lax.broadcasted_iota(jnp.int32, (total, 256), 1).astype(F32)
         cos_x, sin_x = turn_cos_sin(x * x_values, NX)
-        for part, value in enumerate(split(cos_x)):
-            table_ref[part, 0:total, 0:256] = value
-            table_ref[part, total : 2 * total, 256:512] = value
-        for part, value in enumerate(split(sin_x)):
-            table_ref[part, 0:total, 256:512] = value
-            table_ref[part, total : 2 * total, 0:256] = -value
+        cosine, sine = cos_x.astype(BF16), sin_x.astype(BF16)
+        table_ref[0:total, 0:256] = cosine
+        table_ref[total : 2 * total, 256:512] = cosine
+        table_ref[0:total, 256:512] = sine
+        table_ref[total : 2 * total, 0:256] = -sine
 
     for k in range(batch):
         real = turned_ref[pl.ds(group * batch + k, 1), :]
@@ -534,8 +533,7 @@
     amp = amp_ref[...]
     for part in range(2):
         lane = slice(256 * part, 256 * part + 256)
-        result = jnp.dot(amp, table_ref[0, :, lane], preferred_element_type=F32)
-        result = result + jnp.dot(amp, table_ref[1, :, lane], preferred_element_type=F32)
+        result = jnp.dot(amp, table_ref[:, lane], preferred_element_type=F32)
         for k in range(batch):
             out_ref[k, :, part, :] = result[k * y_pad : k * y_pad + y_block, 0:NX]
 
@@ -601,7 +599,7 @@
         functools.partial(mega_kernel, bands, groups),
         in_specs=[hbm] * len(inputs),
         out_specs=vmem,
-        out_shape=jax.ShapeDtypeStruct((devices, stick_rows, lanes), F32),
+        out_shape=pltpu.VMEM((devices, stick_rows, lanes), F32),
         scratch_shapes=[
             pltpu.VMEM(waves.shape, BF16),
             pltpu.VMEM((1, nb), F32),
@@ -615,6 +613,9 @@
             pltpu.VMEM((atoms, 8), F32),
             pltpu.VMEM((HALF, 2 * SPECIES, width), F32),
             pltpu.VMEM((cols, 4 * width), BF16),
+            pltpu.VMEM((3, atoms, 128), F32),
+            pltpu.VMEM((2, atoms, 128), jnp.int32),
+            pltpu.VMEM((3, block, width), F32),
             pltpu.VMEM((HALF * block, 4 * width), BF16),
             pltpu.VMEM((steps, HALF, block, cols), F32),
             pltpu.VMEM((chips, HALF, own, cols), F32),
@@ -634,15 +635,8 @@
             pltpu.VMEM((slots, 2 * half), F32),
             pltpu.VMEM((groups, stick_rows, lanes), F32),
             dma((chips,)),
-            dma((chips,)),
-            dma((chips,)),
-            dma((chips,)),
-            dma((bands,)),
-            dma((bands,)),
-            dma((groups,)),
-            dma((groups,)),
-            dma((devices,)),
-            dma((devices,)),
+            dma((5,)),
+            dma((5,)),
             dma((len(inputs),)),
         ],
         compiler_params=pltpu.CompilerParams(collective_id=0, has_side_effects=True),
@@ -655,17 +649,17 @@
     result = pl.pallas_call(
         functools.partial(finish_kernel, bands, planes, span),
         grid=(planes // batch,),
-        in_specs=[pl.BlockSpec((devices * stick_rows, lanes), lambda g: (0, 0))],
+        in_specs=[vmem],
         out_specs=pl.BlockSpec((batch, y_block, 2, NX), lambda g: (g, 0, 0, 0)),
         out_shape=jax.ShapeDtypeStruct((planes, y_block, 2, NX), F32),
         scratch_shapes=[
-            pltpu.VMEM((2, 2 * total, 512), BF16),
+            pltpu.VMEM((2 * total, 512), BF16),
             pltpu.VMEM((span, total), F32),
             pltpu.VMEM((2, y_pad, total), F32),
             pltpu.VMEM((batch * y_pad, 2 * total), BF16),
         ],
         name="finish",
-    )(received.reshape(devices * stick_rows, lanes))
+    )(pltpu.with_memory_space_constraint(received, pltpu.VMEM))
     return result.transpose(2, 0, 1, 3)
 
 

time: 40 us -> 36.7 us (0.918)
  Pallas kernels: 39.8 us -> 36.5 us
    pallas_call x1, Pallas kernels: 34.2 us -> 32.5 us  [on_device(): pl.pallas_call(functools.partial(mega_kernel, bands, groups), in_specs=[h...]
    pallas_call x1, Pallas kernels: 5.61 us -> 4 us  [on_device(): pl.pallas_call(functools.partial(finish_kernel, bands, planes, span), gri...]
where the time goes in v2:
time: 36.7 us; the launch traced here: 36.5 us
  Pallas kernels  36.5 us (99%)
    pallas_call x1, Pallas kernels, on_device(): pl.pallas_call(functools.partial(mega_kernel, bands, groups), in_specs=[h...  32.5 us
    pallas_call x1, Pallas kernels, on_device(): pl.pallas_call(functools.partial(finish_kernel, bands, planes, span), gri...  4 us

profile of v2, /device:TPU:0, one launch (start us, length us, event | category | flops | bytes accessed | tf_op | source)
XLA Modules:
  0.0 36.5 jit_solution(13923703327225317981)
XLA Ops:
  0.0 32.5 %slots.1.received_ref = f32[32,4,128]{2,1,0:T(4,128)S(1)} custom-call(bf16[2,32,1024]{2,1,0:T(8,128)(2,1)} %waves_hbm.1, f32[1,32]{1,0:T(1,128)} %bitcast.4, f32[72,1024]{1,0:T(8,128)} %beta_hbm.1, s32[3,1024]{1,0:T(4,128)} %miller_hbm.1, s32[1,256]{1,0:T(1,128)} %bitcast.3, s32[3,256]{1,0:T(4,128)} %site_hbm.1, s32[8]{0:T(128)} %columns_hbm.1, ...), custom_call_target="tpu_custom_call" | custom-call | tf_op jit(solution)/shard_map/slots/pallas_call | solution.py:598
  32.5 4.0 %finish.1 = f32[28,60,2,240]{3,2,1,0:T(2,128)} custom-call(f32[32,4,128]{2,1,0:T(4,128)S(1)} %slots.1.received_ref), custom_call_target="tpu_custom_call" | custom-call | tf_op jit(solution)/shard_map/finish/pallas_call | solution.py:649

commit v3 on v2

--- a/solution.py
+++ b/solution.py
@@ -376,42 +376,49 @@
         [pair_ref[q * chunk : (q + 1) * chunk, :] for q in range(chunks)], axis=1
     )
 
-    def band_copy(step):
+    halves = 2 if chunk % 16 == 0 else 1
+    share = chunk // halves
+
+    def band_copy(step, part):
         return pltpu.make_async_remote_copy(
-            src_ref=pack_ref,
-            dst_ref=band_ref.at[band],
-            send_sem=sent.at[2],
-            recv_sem=came.at[2],
+            src_ref=pack_ref.at[pl.ds(part * share, share)],
+            dst_ref=band_ref.at[part, band],
+            send_sem=sent.at[2 + part],
+            recv_sem=came.at[2 + part],
             device_id=(mixed(band, step, bands), me),
             device_id_type=MESH,
         )
 
-    for step in range(bands - 1, 0, -1):
-        band_copy(step).start()
-    summed = pack_ref[...]
-    all_of(2, band_ref, bands - 1).wait_recv()
-    for step in range(1, bands):
-        summed = summed + band_ref[lax.rem(band + step, bands)]
-    sum_ref[...] = summed
-
-    def ga_copy(step):
+    def ga_copy(step, part):
         return pltpu.make_async_remote_copy(
-            src_ref=sum_ref,
-            dst_ref=all_ref.at[me],
-            send_sem=sent.at[3],
-            recv_sem=came.at[3],
+            src_ref=sum_ref.at[pl.ds(part * share, share)],
+            dst_ref=all_ref.at[part, me],
+            send_sem=sent.at[4 + part],
+            recv_sem=came.at[4 + part],
             device_id=(band, mixed(me, step, groups)),
             device_id_type=MESH,
         )
 
-    for step in range(groups - 1, 0, -1):
-        ga_copy(step).start()
-    all_ref[me] = sum_ref[...]
-    all_of(3, all_ref, groups - 1).wait_recv()
+    for part in range(halves):
+        for step in range(bands - 1, 0, -1):
+            band_copy(step, part).start()
+    for part in range(halves):
+        rows_here = slice(part * share, (part + 1) * share)
+        summed = pack_ref[rows_here, :]
+        all_of(2 + part, band_ref.at[part], bands - 1).wait_recv()
+        for step in range(1, bands):
+            summed = summed + band_ref[part, lax.rem(band + step, bands)]
+        sum_ref[rows_here, :] = summed
+        all_ref[part, me] = summed
+        for step in range(groups - 1, 0, -1):
+            ga_copy(step, part).start()
+    for part in range(halves):
+        all_of(4 + part, all_ref.at[part], groups - 1).wait_recv()
     becsum = jnp.concatenate(
         [
-            jnp.concatenate([all_ref[g, :, q * own : (q + 1) * own] for g in range(groups)], axis=1)
+            jnp.concatenate([all_ref[part, g, :, q * own : (q + 1) * own] for g in range(groups)], axis=1)
             for q in range(chunks)
+            for part in range(halves)
         ],
         axis=0,
     )[:pairs]
@@ -462,8 +469,8 @@
         return pltpu.make_async_remote_copy(
             src_ref=stick_ref.at[target[1]],
             dst_ref=out_ref.at[place],
-            send_sem=sent.at[4],
-            recv_sem=came.at[4],
+            send_sem=sent.at[6],
+            recv_sem=came.at[6],
             device_id=target,
             device_id_type=MESH,
         )
@@ -479,63 +486,68 @@
 
     out_ref[place] = stick_ref[me]
 
-    all_of(4, out_ref, devices - 1).wait_recv()
+    all_of(6, out_ref, devices - 1).wait_recv()
 
     all_of(0, mate_ref, chips).wait_send()
     all_of(1, recv_ref, chips - 1).wait_send()
-    all_of(2, band_ref, bands - 1).wait_send()
-    all_of(3, all_ref, groups - 1).wait_send()
-    all_of(4, out_ref, devices - 1).wait_send()
-
-
-def finish_kernel(bands, planes, span, received_ref, out_ref, table_ref, turned_ref, angle_ref, amp_ref):
+    for part in range(halves):
+        all_of(2 + part, band_ref.at[part], bands - 1).wait_send()
+        all_of(4 + part, all_ref.at[part], groups - 1).wait_send()
+    all_of(6, out_ref, devices - 1).wait_send()
+
+
+def finish_kernel(bands, planes, span, received_ref, out_hbm, table_ref, turned_ref, angle_ref, amp_ref, out_ref, sem):
     senders, stick_rows, lanes = received_ref.shape
     per_row = lanes // span
     total = senders * stick_rows * per_row
-    batch = out_ref.shape[0]
-    y_block = out_ref.shape[1]
+    _, batch, y_block, _, _ = out_ref.shape
     y_pad = angle_ref.shape[1]
     band = lax.axis_index("band")
-    group = pl.program_id(0)
-
-    @pl.when(group == 0)
-    def _():
-        received = received_ref[...].reshape(senders * stick_rows, lanes)
-        received = jnp.concatenate([received[:, q * span : (q + 1) * span] for q in range(per_row)], axis=0)
-        turned = jnp.swapaxes(received, 0, 1)
-        turned_ref[...] = turned
-        column_row = turned[2 * planes : 2 * planes + 1, :]
-        live_row = column_row >= 0.0
-        x_row = jnp.floor((column_row + 0.5) * (1.0 / NY))
-        y_row = column_row - x_row * NY
-        y_values = lax.broadcasted_iota(jnp.int32, (y_pad, total), 0) + band * y_block
-        cos_y, sin_y = turn_cos_sin(y_values.astype(F32) * y_row, NY)
-        angle_ref[0] = jnp.where(live_row, cos_y, 0.0)
-        angle_ref[1] = jnp.where(live_row, sin_y, 0.0)
-        column = received[:, 2 * planes : 2 * planes + 1]
-        owner = lax.rem(lax.broadcasted_iota(jnp.int32, (total, 1), 0), total // per_row) // (total // per_row // bands)
-        x = jnp.floor((column + 0.5) * (1.0 / NY)) + owner.astype(F32) * (NX // bands)
-        x_values = lax.broadcasted_iota(jnp.int32, (total, 256), 1).astype(F32)
-        cos_x, sin_x = turn_cos_sin(x * x_values, NX)
-        cosine, sine = cos_x.astype(BF16), sin_x.astype(BF16)
-        table_ref[0:total, 0:256] = cosine
-        table_ref[total : 2 * total, 256:512] = cosine
-        table_ref[0:total, 256:512] = sine
-        table_ref[total : 2 * total, 0:256] = -sine
-
-    for k in range(batch):
-        real = turned_ref[pl.ds(group * batch + k, 1), :]
-        imag = turned_ref[pl.ds(planes + group * batch + k, 1), :]
-        cosine, sine = angle_ref[0], angle_ref[1]
-        row = k * y_pad
-        amp_ref[row : row + y_pad, 0:total] = (real * cosine - imag * sine).astype(BF16)
-        amp_ref[row : row + y_pad, total : 2 * total] = (real * sine + imag * cosine).astype(BF16)
-    amp = amp_ref[...]
-    for part in range(2):
-        lane = slice(256 * part, 256 * part + 256)
-        result = jnp.dot(amp, table_ref[:, lane], preferred_element_type=F32)
+
+    received = received_ref[...].reshape(senders * stick_rows, lanes)
+    received = jnp.concatenate([received[:, q * span : (q + 1) * span] for q in range(per_row)], axis=0)
+    turned = jnp.swapaxes(received, 0, 1)
+    turned_ref[...] = turned
+    column_row = turned[2 * planes : 2 * planes + 1, :]
+    live_row = column_row >= 0.0
+    x_row = jnp.floor((column_row + 0.5) * (1.0 / NY))
+    y_row = column_row - x_row * NY
+    y_values = lax.broadcasted_iota(jnp.int32, (y_pad, total), 0) + band * y_block
+    cos_y, sin_y = turn_cos_sin(y_values.astype(F32) * y_row, NY)
+    angle_ref[0] = jnp.where(live_row, cos_y, 0.0)
+    angle_ref[1] = jnp.where(live_row, sin_y, 0.0)
+    column = received[:, 2 * planes : 2 * planes + 1]
+    owner = lax.rem(lax.broadcasted_iota(jnp.int32, (total, 1), 0), total // per_row) // (total // per_row // bands)
+    x = jnp.floor((column + 0.5) * (1.0 / NY)) + owner.astype(F32) * (NX // bands)
+    x_values = lax.broadcasted_iota(jnp.int32, (total, 256), 1).astype(F32)
+    cos_x, sin_x = turn_cos_sin(x * x_values, NX)
+    cosine, sine = cos_x.astype(BF16), sin_x.astype(BF16)
+    table_ref[0:total, 0:256] = cosine
+    table_ref[total : 2 * total, 256:512] = cosine
+    table_ref[0:total, 256:512] = sine
+    table_ref[total : 2 * total, 0:256] = -sine
+
+    def copy(n):
+        return pltpu.make_async_copy(out_ref.at[n % 2], out_hbm.at[pl.ds(n * batch, batch)], sem.at[n % 2])
+
+    for n in range(planes // batch):
         for k in range(batch):
-            out_ref[k, :, part, :] = result[k * y_pad : k * y_pad + y_block, 0:NX]
+            plane = n * batch + k
+            real, imag = turned_ref[plane : plane + 1, :], turned_ref[planes + plane : planes + plane + 1, :]
+            cosine, sine = angle_ref[0], angle_ref[1]
+            row = k * y_pad
+            amp_ref[row : row + y_pad, 0:total] = (real * cosine - imag * sine).astype(BF16)
+            amp_ref[row : row + y_pad, total : 2 * total] = (real * sine + imag * cosine).astype(BF16)
+        amp = amp_ref[...]
+        if n >= 2:
+            copy(n - 2).wait()
+        for part in range(2):
+            result = jnp.dot(amp, table_ref[:, 256 * part : 256 * part + 256], preferred_element_type=F32)
+            for k in range(batch):
+                out_ref[n % 2, k, :, part, :] = result[k * y_pad : k * y_pad + y_block, 0:NX]
+        copy(n).start()
+    for n in range(max(0, planes // batch - 2), planes // batch):
+        copy(n).wait()
 
 
 def on_device(
@@ -561,6 +573,7 @@
     stick_rows = slots * span // lanes
     chunks = 128 // own
     chunk = up(-(-pairs // chunks), 8)
+    halves = 2 if chunk % 16 == 0 else 1
 
     odd = (ELL[PAIR_FIRST] + ELL[PAIR_SECOND]) % 2 == 1
     factors = np.where(PAIR_FIRST == PAIR_SECOND, 1.0, 2.0)
@@ -623,11 +636,11 @@
             pltpu.VMEM((points // tile, 2, atoms, tile), F32),
             pltpu.VMEM((up(HALF * own, 128), cols), F32),
             pltpu.VMEM((up(NH, 8), part_lanes), F32),
-            pltpu.VMEM((bands, chunk, chunks * own), F32),
+            pltpu.VMEM((halves, bands, chunk // halves, chunks * own), F32),
             pltpu.VMEM((chunk * chunks, own), F32),
             pltpu.VMEM((chunk, chunks * own), F32),
             pltpu.VMEM((chunk, chunks * own), F32),
-            pltpu.VMEM((groups, chunk, chunks * own), F32),
+            pltpu.VMEM((halves, groups, chunk // halves, chunks * own), F32),
             pltpu.VMEM((up(SPECIES * pairs, 128), 2 * atoms), F32),
             pltpu.VMEM(aug_table.shape, BF16),
             pltpu.VMEM((2,) + spread.shape, BF16),
@@ -635,8 +648,8 @@
             pltpu.VMEM((slots, 2 * half), F32),
             pltpu.VMEM((groups, stick_rows, lanes), F32),
             dma((chips,)),
-            dma((5,)),
-            dma((5,)),
+            dma((7,)),
+            dma((7,)),
             dma((len(inputs),)),
         ],
         compiler_params=pltpu.CompilerParams(collective_id=0, has_side_effects=True),
@@ -644,19 +657,20 @@
     )(*inputs)
     y_block = NY // bands
     total = devices * slots
-    batch = math.gcd(planes, 7)
+    batch = math.gcd(planes, 14)
     y_pad = up(y_block, 16)
     result = pl.pallas_call(
         functools.partial(finish_kernel, bands, planes, span),
-        grid=(planes // batch,),
         in_specs=[vmem],
-        out_specs=pl.BlockSpec((batch, y_block, 2, NX), lambda g: (g, 0, 0, 0)),
+        out_specs=hbm,
         out_shape=jax.ShapeDtypeStruct((planes, y_block, 2, NX), F32),
         scratch_shapes=[
             pltpu.VMEM((2 * total, 512), BF16),
             pltpu.VMEM((span, total), F32),
             pltpu.VMEM((2, y_pad, total), F32),
             pltpu.VMEM((batch * y_pad, 2 * total), BF16),
+            pltpu.VMEM((2, batch, y_block, 2, NX), F32),
+            dma((2,)),
         ],
         name="finish",
     )(pltpu.with_memory_space_constraint(received, pltpu.VMEM))

time: 36.7 us -> 35.5 us (0.967)
  Pallas kernels: 36.5 us -> 35.3 us
    pallas_call x1, Pallas kernels: 4 us -> 3.31 us  [on_device(): pl.pallas_call(functools.partial(finish_kernel, bands, planes, span), in_...]
    pallas_call x1, Pallas kernels: 32.5 us -> 32 us  [on_device(): pl.pallas_call(functools.partial(mega_kernel, bands, groups), in_specs=[h...]
where the time goes in v3:
time: 35.5 us; the launch traced here: 35.4 us
  Pallas kernels  35.3 us (99%)
    pallas_call x1, Pallas kernels, on_device(): pl.pallas_call(functools.partial(mega_kernel, bands, groups), in_specs=[h...  32 us
    pallas_call x1, Pallas kernels, on_device(): pl.pallas_call(functools.partial(finish_kernel, bands, planes, span), in_...  3.31 us

profile of v3, /device:TPU:0, one launch (start us, length us, event | category | flops | bytes accessed | tf_op | source)
XLA Modules:
  0.0 35.4 jit_solution(2746887160765233660)
XLA Ops:
  0.0 32.0 %slots.1.received_ref = f32[32,4,128]{2,1,0:T(4,128)S(1)} custom-call(bf16[2,32,1024]{2,1,0:T(8,128)(2,1)} %waves_hbm.1, f32[1,32]{1,0:T(1,128)} %bitcast.4, f32[72,1024]{1,0:T(8,128)} %beta_hbm.1, s32[3,1024]{1,0:T(4,128)} %miller_hbm.1, s32[1,256]{1,0:T(1,128)} %bitcast.3, s32[3,256]{1,0:T(4,128)} %site_hbm.1, s32[8]{0:T(128)} %columns_hbm.1, ...), custom_call_target="tpu_custom_call" | custom-call | tf_op jit(solution)/shard_map/slots/pallas_call | solution.py:611
  32.0 3.3 %finish.1 = f32[28,60,2,240]{3,2,1,0:T(2,128)} custom-call(f32[32,4,128]{2,1,0:T(4,128)S(1)} %slots.1.received_ref), custom_call_target="tpu_custom_call" | custom-call | tf_op jit(solution)/shard_map/finish/pallas_call | solution.py:662
